TPU v7x, 8 devices: a whole 2x2x1 slice. The times are simulated.
8 devices in a mesh: dp: 2 (over z, y), fsdp: 4 (over x, core).
Axes of the slice: x: 2, y: 2, z: 1, core: 2. Of those that a mesh axis runs over, the one named last changes fastest.
Arguments:
- hidden: bfloat16 [8192, 512], P(('dp', 'fsdp')), parts along dimension 0
- targets: int32 [8192], P(('dp', 'fsdp')), parts along dimension 0
- weight: bfloat16 [32128, 512], P('fsdp')
Outputs:
- output 1: float32 [2], P('dp'), parts along dimension 0
- output 2: float32 [8192, 512], P(('dp', 'fsdp')), parts along dimension 0
- output 3: float32 [64256, 512], P(('dp', 'fsdp')), parts along dimension 0
There are 2 independent parts. A program takes and returns all parts, laid end to end along the dimension named above; an argument that names none is the same for every part.
All inputs are finite; a program needn't handle non-finite values.
Results may differ from a plain program's by a relative error of at most 0.001.
Values are sent between devices in bfloat16 or wider.
A program may use at most 1 GiB of HBM per device.

v0:
```python
import jax
import jax.numpy as jnp
from jax import lax
from jax.experimental import pallas as pl
from jax.experimental.pallas import tpu as pltpu
from jax.sharding import PartitionSpec as P

SUB = 256
UN_O = 4
UN_F = 14
UN_B = 14
UN_L = 4
f32 = jnp.float32
bf16 = jnp.bfloat16
MESH = pl.DeviceIdType.MESH


def _nn(a, b):
    return lax.dot_general(a, b, (((1,), (0,)), ((), ())), preferred_element_type=f32)


def _tn(a, b):
    return lax.dot_general(a, b, (((0,), (0,)), ((), ())), preferred_element_type=f32)


def _pieces(full, rem, unroll):
    loops = (full - 2) // unroll
    cuts = [0, 2 * SUB] + [(2 + (i + 1) * unroll) * SUB for i in range(loops)] + [full * SUB + rem]
    return [(a, b - a) for a, b in zip(cuts[:-1], cuts[1:])]


def _fwd_chunk(w, h, ht, zb, mb, s8, un, tgt=None, zt8=None, mid=None, need=None, clear=None):
    vloc = w.shape[0]
    tok = h.shape[0]
    full, rem = vloc // SUB, vloc % SUB
    loops = (full - 2) // un
    ht[...] = h[...].T
    mb[1][...] = jnp.full(mb[1].shape, -jnp.inf, f32)
    s8[...] = jnp.zeros(s8.shape, f32)

    def zdot(k, slot, rows=SUB):
        z = _nn(w[pl.ds(k * SUB, rows), :], ht[...])
        zb[slot][pl.ds(0, rows), :] = z
        mb[slot][...] = jnp.maximum(mb[1 - slot][...], jnp.max(z.reshape(rows // 8, 8, tok), axis=0))

    def epi(k, slot, rows=SUB):
        z = zb[slot][pl.ds(0, rows), :].reshape(rows // 8, 8, tok)
        new = mb[slot][...]
        s8[...] = s8[...] * jnp.exp(mb[2][...] - new) + jnp.sum(jnp.exp(z - new[None]), axis=0)
        mb[2][...] = new
        if clear is not None:
            clear[pl.ds(k * SUB, rows), :] = jnp.zeros((rows, clear.shape[1]), f32)
        if tgt is not None:
            t = tgt - k * SUB
            lane = lax.broadcasted_iota(jnp.int32, (8, tok), 0)
            acc = zt8[...]
            for r in range(rows // 8):
                acc = jnp.where(lane + r * 8 == t, z[r], acc)
            zt8[...] = acc

    def step(k, par, zrows=SUB, erows=SUB):
        if zrows:
            zdot(k + 1, 1 - par, zrows)
        if erows:
            epi(k, par, erows)

    mb[2][...] = mb[1][...]
    if need is not None:
        need(0)
    zdot(0, 0)
    step(0, 0)

    @pl.loop(0, loops)
    def _(i):
        if need is not None:
            for n in range(loops):
                pl.when(i == n)(lambda n=n: need(1 + n))
        for u in range(un):
            step(1 + i * un + u, (1 + u) % 2)
        if mid is not None:
            pl.when(i == 0)(mid)

    if need is not None:
        need(1 + loops)
    for k in range(1 + loops * un, full - 1):
        step(k, k % 2)
    step(full - 1, (full - 1) % 2, zrows=rem)
    step(full, full % 2, zrows=0, erows=rem)
    m8 = mb[2][...]
    top = jnp.max(m8, axis=0, keepdims=True)
    return top + jnp.log(jnp.sum(s8[...] * jnp.exp(m8 - top), axis=0, keepdims=True))


def _bwd_chunk(w, h, ht, lse, tgt, dw, dht, zb, gb, un, zt8=None, mid=None, need=None, done=None, scale=1.0):
    vloc = w.shape[0]
    tok = h.shape[0]
    full, rem = vloc // SUB, vloc % SUB
    loops = (full - 2) // un

    def zdot(k, slot, rows=SUB):
        zb[slot][pl.ds(0, rows), :] = _nn(w[pl.ds(k * SUB, rows), :], ht[...])

    def epi(k, slot, rows=SUB):
        z = zb[slot][pl.ds(0, rows), :]
        hit = lax.broadcasted_iota(jnp.int32, (rows, tok), 0) == tgt[...] - k * SUB
        p = jnp.exp(z - lse[...])
        if zt8 is not None:
            zt8[...] += jnp.sum(jnp.where(hit, z, 0.0).reshape(rows // 8, 8, tok), axis=0)
        gb[slot][pl.ds(0, rows), :] = ((p - jnp.where(hit, 1.0, 0.0)) * scale).astype(bf16)

    def ddot(k, slot, rows=SUB):
        g = gb[slot][pl.ds(0, rows), :]
        rng = pl.ds(k * SUB, rows)
        dw[rng, :] = dw[rng, :] + _nn(g, h[...])
        dht[...] += _tn(w[rng, :], g)

    def step(k, par, zrows=SUB, erows=SUB, drows=SUB):
        if drows:
            ddot(k - 1, 1 - par, drows)
        if zrows:
            zdot(k + 1, 1 - par, zrows)
        if erows:
            epi(k, par, erows)

    dht[...] = jnp.zeros(dht.shape, f32)
    if need is not None:
        need(0)
    zdot(0, 0)
    step(0, 0, drows=0)
    if mid is not None:
        mid()

    @pl.loop(0, loops)
    def _(i):
        if need is not None:
            for n in range(loops):
                pl.when(i == n)(lambda n=n: need(1 + n))
        for u in range(un):
            step(1 + i * un + u, (1 + u) % 2)
        if done is not None:
            for n in range(loops):
                done(n, i == n)

    if need is not None:
        need(1 + loops)
    for k in range(1 + loops * un, full - 1):
        step(k, k % 2)
    step(full - 1, (full - 1) % 2, zrows=rem)
    step(full, full % 2, zrows=0, erows=rem)
    step(full + 1, (full + 1) % 2, zrows=0, erows=0, drows=rem)
    if done is not None:
        done(loops, None)


def _done_pieces(vloc, un):
    full = vloc // SUB
    loops = (full - 2) // un
    cuts = [0] + [(i + 1) * un * SUB for i in range(loops)] + [vloc]
    return [(a, b - a) for a, b in zip(cuts[:-1], cuts[1:])]


def _exchange_kernel(total, h_in, t_in, w_in, dwp, x_out, s_out, lse_out, loss_out,
                     w, hc, ht, dw, dht, part, ring, tg, lst, zs, lsec, z0, z1, g0, g1, ma, mb_, mc, s8, zt8, ztf,
                     wsem, lsem, hsend, hrecv, tsend, trecv, stsend, strecv, psend, precv, zsend, zrecv, osem):
    vloc, depth = w_in.shape
    tok = h_in.shape[0]
    half = tok // 2
    me = lax.axis_index("fsdp")
    chip, core = me // 2, me % 2
    sib = 2 * chip + (1 - core)
    far = 2 * (1 - chip) + core
    fars = [2 * (1 - chip), 2 * (1 - chip) + 1]
    base = me * vloc
    dev = lambda d: {"fsdp": d}
    zb, gb, mb = (z0, z1), (g0, g1), (ma, mb_, mc)
    scale = 1.0 / total

    def rcopy(src, dst, ssem, rsem, d):
        return pltpu.make_async_remote_copy(src_ref=src, dst_ref=dst, send_sem=ssem, recv_sem=rsem, device_id=dev(d), device_id_type=MESH)

    def wait_bytes(ref, sem):
        pltpu.make_async_copy(ref, ref, sem).wait()

    pieces = _pieces(vloc // SUB, vloc % SUB, UN_O)
    wcopy = [pltpu.make_async_copy(w_in.at[pl.ds(a, n), :], w.at[pl.ds(a, n), :], wsem.at[i]) for i, (a, n) in enumerate(pieces)]
    own_h = pltpu.make_async_copy(h_in, hc.at[0], lsem.at[0])
    own_t = pltpu.make_async_copy(t_in, tg.at[pl.ds(0, 2)], lsem.at[1])
    own_h.start()
    own_t.start()
    for c in wcopy:
        c.start()

    barrier = pltpu.get_barrier_semaphore()
    for d in [sib] + fars:
        pl.semaphore_signal(barrier, inc=1, device_id=dev(d), device_id_type=MESH)
    pl.semaphore_wait(barrier, 3)

    mine = pl.ds(core * half, half)
    send_sib = rcopy(h_in, hc.at[1], hsend.at[0], hrecv.at[0], sib)
    send_far = [rcopy(h_in.at[pl.ds(i * half, half), :], hc.at[2 + i, mine, :], hsend.at[1 + i], hrecv.at[1 + i], far) for i in range(2)]
    relay = [rcopy(hc.at[2 + i, mine, :], hc.at[2 + i, mine, :], hsend.at[3 + i], hrecv.at[3 + i], sib) for i in range(2)]
    send_sib.start()
    for c in send_far:
        c.start()
    rcopy(t_in, tg.at[pl.ds(2, 2)], tsend, trecv, sib).start()
    for d in fars:
        for i in range(2):
            rcopy(t_in.at[pl.ds(i, 1)], tg.at[pl.ds(4 + 2 * i + core, 1)], tsend, trecv, d).start()

    zt8[...] = jnp.zeros(zt8.shape, f32)
    ztf[...] = jnp.zeros(ztf.shape, f32)

    def put_stat(pos, v):
        for i in range(2):
            lst[me * 8 + pos * 2 + i] = v[:, i * half:(i + 1) * half]

    def send_stat(pos):
        def go(row, dst_pos, dst_half, d):
            rcopy(lst.at[pl.ds(me * 8 + row, 1)], lst.at[pl.ds(me * 8 + dst_pos * 2 + dst_half, 1)], stsend, strecv.at[dst_pos], d).start()

        near = pos < 2
        for i in range(2):
            go(pos * 2 + i, jnp.where(near, 1 - pos, pos), i, sib)
            for k in range(2):
                go(
                    pos * 2 + i,
                    jnp.where(near, 2 + i, jnp.where(k == i, 0, 1)),
                    jnp.where(near, jnp.where(pos == 0, core, 1 - core), pos - 2),
                    fars[k],
                )

    own_h.wait()
    own_t.wait()
    tg0 = jnp.concatenate([tg[0], tg[1]], axis=1) - base
    put_stat(0, _fwd_chunk(w, hc.at[0], ht.at[0], zb, mb, s8, UN_O, tgt=tg0, zt8=ztf, need=lambda n: wcopy[n].wait(), clear=dw))
    send_stat(0)

    @pl.loop(1, 4)
    def _(pos):
        @pl.when(pos == 1)
        def _():
            send_sib.wait_recv()

        for i in range(2):
            @pl.when(pos == 2 + i)
            def _():
                relay[i].wait_recv()

        def forward():
            for i in range(2):
                @pl.when(pos == 1 + i)
                def _():
                    send_far[i].wait_recv()
                    relay[i].start()

        put_stat(pos, _fwd_chunk(w, hc.at[pos], ht.at[pos], zb, mb, s8, UN_F, mid=forward))
        send_stat(pos)

    wait_bytes(tg.at[pl.ds(2, 6)], trecv)

    def join_stat(pos):
        rows = [[lst[s * 8 + pos * 2 + i] for s in range(4)] for i in range(2)]
        out = []
        for r in rows:
            top = jnp.maximum(jnp.maximum(r[0], r[1]), jnp.maximum(r[2], r[3]))
            out.append(top + jnp.log(sum(jnp.exp(x - top) for x in r)))
        return jnp.concatenate(out, axis=1)

    dpieces = _done_pieces(vloc, UN_B)
    flush = [pltpu.make_async_copy(dw.at[pl.ds(a, n), :], dwp.at[pl.ds(a, n), :], osem.at[i]) for i, (a, n) in enumerate(dpieces)]
    theirs = pl.ds((1 - core) * half, half)
    swap = [rcopy(part.at[i, theirs, :], ring.at[i], psend.at[i], precv.at[i], sib) for i in range(2)]
    cross = [rcopy(part.at[i, mine, :], x_out.at[pl.ds(i * half, half), :], psend.at[2 + i], precv.at[2 + i], far) for i in range(2)]
    last = rcopy(part.at[2], s_out, psend.at[4], precv.at[4], sib)

    lsum = jnp.zeros((1, tok), f32)

    @pl.loop(0, 3)
    def _(i):
        pos = lax.rem(i + 1, 3) + 1
        for q in range(3):
            @pl.when(i == q)
            def _():
                wait_bytes(lst.at[pl.ds(0, 6)], strecv.at[(2, 3, 1)[q]])

        lse = join_stat(pos)
        lsec[pl.ds(pos, 1)] = lse[None]
        tpos = jnp.concatenate([tg[pos * 2], tg[pos * 2 + 1]], axis=1) - base

        def combine():
            for q in range(2):
                @pl.when(i == q + 1)
                def _():
                    swap[q].wait_recv()
                    for j in range(4):
                        rows = pl.ds(core * half + j * (half // 4), half // 4)
                        part[q, rows, :] += ring[q, pl.ds(j * (half // 4), half // 4), :]
                    cross[q].start()

        def done(n, cond):
            pl.when(i == 2 if cond is None else jnp.logical_and(cond, i == 2))(lambda: flush[n].start())

        _bwd_chunk(w, hc.at[pos], ht.at[pos], lse, tpos, dw, dht, zb, gb, UN_B, zt8=zt8, mid=combine, done=done, scale=scale)
        part[i] = dht[...].T
        for q in range(2):
            pl.when(i == q)(lambda q=q: swap[q].start())

    last.start()
    wait_bytes(lst.at[pl.ds(0, 6)], strecv.at[0])
    lsec[0] = join_stat(0)
    lse_out[...] = lsec[0]
    zsum = jnp.sum(zt8[...] + ztf[...], keepdims=True)
    zs[me] = jnp.broadcast_to(zsum, (1, 128))
    for d in [sib] + fars:
        rcopy(zs.at[pl.ds(me, 1)], zs.at[pl.ds(me, 1)], zsend, zrecv, d).start()
    lsum = jnp.sum(lsec[0] + lsec[1] + lsec[2] + lsec[3], keepdims=True)
    wait_bytes(zs.at[pl.ds(0, 3)], zrecv)
    loss_out[...] = (lsum - (zs[0] + zs[1] + zs[2] + zs[3])) * scale
    wait_bytes(zs.at[pl.ds(0, 3)], zsend)
    wait_bytes(lst.at[pl.ds(0, 24)], stsend)
    wait_bytes(tg.at[pl.ds(0, 6)], tsend)
    for c in [send_sib] + send_far + relay + swap:
        c.wait_send()
    for c in flush:
        c.wait()
    for c in cross + [last]:
        c.wait()


def _own_kernel(total, w_in, h_in, t_ref, lse_ref, dwp, x_in, s_in, dwo, dh_ref,
                w, h, ht, xv, sv, dw, dht, z0, z1, g0, g1, wsem, dsem, osem, lsem):
    vloc, depth = w_in.shape
    pieces = _pieces(vloc // SUB, vloc % SUB, UN_L)
    dpieces = _done_pieces(vloc, UN_L)
    wcopy = [pltpu.make_async_copy(w_in.at[pl.ds(a, n), :], w.at[pl.ds(a, n), :], wsem.at[i]) for i, (a, n) in enumerate(pieces)]
    dcopy = [pltpu.make_async_copy(dwp.at[pl.ds(a, n), :], dw.at[pl.ds(a, n), :], dsem.at[i]) for i, (a, n) in enumerate(dpieces)]
    flush = [pltpu.make_async_copy(dw.at[pl.ds(a, n), :], dwo.at[pl.ds(a, n), :], osem.at[i]) for i, (a, n) in enumerate(dpieces)]
    own_h = pltpu.make_async_copy(h_in, h, lsem.at[0])
    recv = [pltpu.make_async_copy(x_in, xv, lsem.at[1]), pltpu.make_async_copy(s_in, sv, lsem.at[2])]
    own_h.start()
    wcopy[0].start()
    for i in range(len(dpieces)):
        wcopy[i + 1].start()
        dcopy[i].start()
    for c in recv:
        c.start()
    own_h.wait()
    ht[...] = h[...].T

    def need(n):
        wcopy[n].wait()
        if n > 0:
            dcopy[n - 1].wait()

    def done(n, cond):
        if cond is None:
            flush[n].start()
        else:
            pl.when(cond)(lambda: flush[n].start())

    tgt = t_ref[...] - lax.axis_index("fsdp") * vloc
    _bwd_chunk(w, h, ht, lse_ref, tgt, dw, dht, (z0, z1), (g0, g1), UN_L, need=need, done=done, scale=1.0 / total)
    for c in recv:
        c.wait()
    dh_ref[...] = dht[...].T + (xv[...] + sv[...])
    for c in flush:
        c.wait()


def solution(mesh):
    groups = mesh.shape["fsdp"]
    tok_spec = P(("dp", "fsdp"), None)

    def local_head(hidden, targets, weight):
        tok, depth = hidden.shape
        vloc = weight.shape[0]
        total = tok * groups
        half = tok // 2
        vm = pltpu.VMEM
        dma = pltpu.SemaphoreType.DMA
        hbm = pl.BlockSpec(memory_space=pl.ANY)
        loc = pl.BlockSpec(memory_space=pltpu.VMEM)
        np_f = len(_pieces(vloc // SUB, vloc % SUB, UN_O))
        np_b = len(_pieces(vloc // SUB, vloc % SUB, UN_L))
        nd = len(_done_pieces(vloc, UN_B))
        nl = len(_done_pieces(vloc, UN_L))
        sds = jax.ShapeDtypeStruct
        dwp, x, s, lse, loss = pl.pallas_call(
            lambda *refs: _exchange_kernel(total, *refs),
            in_specs=[hbm, hbm, hbm],
            out_specs=[hbm, hbm, hbm, loc, loc],
            out_shape=[sds((vloc, depth), f32), sds((tok, depth), f32), sds((tok, depth), f32), sds((1, tok), f32), sds((1, 128), f32)],
            scratch_shapes=[
                vm((vloc, depth), bf16), vm((groups, tok, depth), bf16), vm((groups, depth, tok), bf16), vm((vloc, depth), f32),
                vm((depth, tok), f32), vm((3, tok, depth), f32), vm((2, half, depth), f32),
                vm((8, 1, half), jnp.int32), vm((32, 1, half), f32), vm((4, 1, 128), f32), vm((4, 1, tok), f32),
                vm((SUB, tok), f32), vm((SUB, tok), f32), vm((SUB, tok), bf16), vm((SUB, tok), bf16),
                vm((8, tok), f32), vm((8, tok), f32), vm((8, tok), f32), vm((8, tok), f32), vm((8, tok), f32), vm((8, tok), f32),
                dma((np_f,)), dma((2,)), dma((5,)), dma((5,)), dma, dma, dma, dma((4,)), dma((5,)), dma((5,)), dma, dma, dma((nd,)),
            ],
            compiler_params=pltpu.CompilerParams(vmem_limit_bytes=66_500_000, collective_id=0, has_side_effects=True),
            name="ce_exchange",
        )(hidden, targets.reshape(2, 1, half), weight)
        dw, dh = pl.pallas_call(
            lambda *refs: _own_kernel(total, *refs),
            in_specs=[hbm, hbm, loc, loc, hbm, hbm, hbm],
            out_specs=[hbm, loc],
            out_shape=[sds((vloc, depth), f32), sds((tok, depth), f32)],
            scratch_shapes=[
                vm((vloc, depth), bf16), vm((tok, depth), bf16), vm((depth, tok), bf16), vm((tok, depth), f32), vm((tok, depth), f32),
                vm((vloc, depth), f32), vm((depth, tok), f32),
                vm((SUB, tok), f32), vm((SUB, tok), f32), vm((SUB, tok), bf16), vm((SUB, tok), bf16),
                dma((np_b,)), dma((nl,)), dma((nl,)), dma((3,)),
            ],
            compiler_params=pltpu.CompilerParams(vmem_limit_bytes=66_500_000),
            name="ce_own",
        )(weight, hidden, targets[None, :], lse, dwp, x, s)
        return loss[0, :1], dh, dw

    return jax.shard_map(local_head, mesh=mesh, in_specs=(tok_spec, P(("dp", "fsdp")), P("fsdp", None)), out_specs=(P("dp"), tok_spec, tok_spec), check_vma=False)
```

profile of v0, /device:TPU:0, one launch (start us, length us, event | category | flops | bytes accessed | tf_op | source)
XLA Modules:
  0.0 185.1 jit_solution(7049482589787357620)
XLA Ops:
  0.6 144.8 %ce_exchange.1 = (f32[8032,512]{1,0:T(8,128)}, f32[1024,512]{1,0:T(8,128)}, f32[1024,512]{1,0:T(8,128)}, f32[1,1024]{1,0:T(1,128)}, f32[1,128]{1,0:T(1,128)}) custom-call(bf16[1024,512]{1,0:T(8,128)(2,1)} %refs_1_.1, s32[2,1,512]{2,1,0:T(1,128)} %bitcast.4, bf16[8032,512]{1,0:T(8,128)(2,1)} %refs_0_.3), custom_call_target="tpu_custom_call" | custom-call | tf_op jit(solution)/shard_map/ce_exchange/pallas_call | solution.py:388
  145.4 0.0 copy-start
  145.4 38.6 %ce_own.1 = (f32[8032,512]{1,0:T(8,128)}, f32[1024,512]{1,0:T(8,128)}) custom-call(bf16[8032,512]{1,0:T(8,128)(2,1)} %refs_0_.3, bf16[1024,512]{1,0:T(8,128)(2,1)} %refs_1_.1, s32[1,1024]{1,0:T(1,128)} %bitcast.5, f32[1,1024]{1,0:T(1,128)} %get-tuple-element.11.refs_3_, f32[8032,512]{1,0:T(8,128)} %get-tuple-element.12.refs_4_, ...), custom_call_target="tpu_custom_call" | custom-call | tf_op jit(solution)/shard_map/ce_own/pallas_call | solution.py:404
  184.0 0.0 copy-done
Async XLA Ops:
  145.4 38.6 %copy-start = (f32[1,128]{1,0:T(1,128)S(1)}, f32[1,128]{1,0:T(1,128)}, u32[]{:S(2)}) copy-start(f32[1,128]{1,0:T(1,128)} %get-tuple-element.10) | copy-start | bytes 1540
where the time goes:
time: 185 us
  Pallas kernels  183 us (99%)
    pallas_call x1, Pallas kernels, local_head(): pl.pallas_call(lambda *refs: _exchange_kernel(total, *refs), in_specs=[hb...  145 us
    pallas_call x1, Pallas kernels, local_head(): pl.pallas_call(lambda *refs: _own_kernel(total, *refs), in_specs=[hbm, hb...  38.6 us

commit v1 on v0

--- a/solution.py
+++ b/solution.py
@@ -10,6 +10,8 @@
 UN_F = 14
 UN_B = 14
 UN_L = 4
+VMEM_X = 44_000_000
+VMEM_L = 30_000_000
 f32 = jnp.float32
 bf16 = jnp.bfloat16
 MESH = pl.DeviceIdType.MESH
@@ -159,8 +161,8 @@
     return [(a, b - a) for a, b in zip(cuts[:-1], cuts[1:])]
 
 
-def _exchange_kernel(total, h_in, t_in, w_in, dwp, x_out, s_out, lse_out, loss_out,
-                     w, hc, ht, dw, dht, part, ring, tg, lst, zs, lsec, z0, z1, g0, g1, ma, mb_, mc, s8, zt8, ztf,
+def _exchange_kernel(total, h_in, t_in, w_in, dwp, w, h0, x_out, s_out, lse_out, loss_out,
+                     dw, hc, ht0, ht, dht, part, ring, tg, lst, zs, lsec, z0, z1, g0, g1, ma, mb_, mc, s8, zt8, ztf,
                      wsem, lsem, hsend, hrecv, tsend, trecv, stsend, strecv, psend, precv, zsend, zrecv, osem):
     vloc, depth = w_in.shape
     tok = h_in.shape[0]
@@ -183,7 +185,7 @@
 
     pieces = _pieces(vloc // SUB, vloc % SUB, UN_O)
     wcopy = [pltpu.make_async_copy(w_in.at[pl.ds(a, n), :], w.at[pl.ds(a, n), :], wsem.at[i]) for i, (a, n) in enumerate(pieces)]
-    own_h = pltpu.make_async_copy(h_in, hc.at[0], lsem.at[0])
+    own_h = pltpu.make_async_copy(h_in, h0, lsem.at[0])
     own_t = pltpu.make_async_copy(t_in, tg.at[pl.ds(0, 2)], lsem.at[1])
     own_h.start()
     own_t.start()
@@ -196,9 +198,9 @@
     pl.semaphore_wait(barrier, 3)
 
     mine = pl.ds(core * half, half)
-    send_sib = rcopy(h_in, hc.at[1], hsend.at[0], hrecv.at[0], sib)
-    send_far = [rcopy(h_in.at[pl.ds(i * half, half), :], hc.at[2 + i, mine, :], hsend.at[1 + i], hrecv.at[1 + i], far) for i in range(2)]
-    relay = [rcopy(hc.at[2 + i, mine, :], hc.at[2 + i, mine, :], hsend.at[3 + i], hrecv.at[3 + i], sib) for i in range(2)]
+    send_sib = rcopy(h_in, hc.at[0], hsend.at[0], hrecv.at[0], sib)
+    send_far = [rcopy(h_in.at[pl.ds(i * half, half), :], hc.at[1 + i, mine, :], hsend.at[1 + i], hrecv.at[1 + i], far) for i in range(2)]
+    relay = [rcopy(hc.at[1 + i, mine, :], hc.at[1 + i, mine, :], hsend.at[3 + i], hrecv.at[3 + i], sib) for i in range(2)]
     send_sib.start()
     for c in send_far:
         c.start()
@@ -232,7 +234,7 @@
     own_h.wait()
     own_t.wait()
     tg0 = jnp.concatenate([tg[0], tg[1]], axis=1) - base
-    put_stat(0, _fwd_chunk(w, hc.at[0], ht.at[0], zb, mb, s8, UN_O, tgt=tg0, zt8=ztf, need=lambda n: wcopy[n].wait(), clear=dw))
+    put_stat(0, _fwd_chunk(w, h0, ht0, zb, mb, s8, UN_O, tgt=tg0, zt8=ztf, need=lambda n: wcopy[n].wait(), clear=dw))
     send_stat(0)
 
     @pl.loop(1, 4)
@@ -253,7 +255,7 @@
                     send_far[i].wait_recv()
                     relay[i].start()
 
-        put_stat(pos, _fwd_chunk(w, hc.at[pos], ht.at[pos], zb, mb, s8, UN_F, mid=forward))
+        put_stat(pos, _fwd_chunk(w, hc.at[pos - 1], ht.at[pos - 1], zb, mb, s8, UN_F, mid=forward))
         send_stat(pos)
 
     wait_bytes(tg.at[pl.ds(2, 6)], trecv)
@@ -300,7 +302,7 @@
         def done(n, cond):
             pl.when(i == 2 if cond is None else jnp.logical_and(cond, i == 2))(lambda: flush[n].start())
 
-        _bwd_chunk(w, hc.at[pos], ht.at[pos], lse, tpos, dw, dht, zb, gb, UN_B, zt8=zt8, mid=combine, done=done, scale=scale)
+        _bwd_chunk(w, hc.at[pos - 1], ht.at[pos - 1], lse, tpos, dw, dht, zb, gb, UN_B, zt8=zt8, mid=combine, done=done, scale=scale)
         part[i] = dht[...].T
         for q in range(2):
             pl.when(i == q)(lambda q=q: swap[q].start())
@@ -327,30 +329,11 @@
         c.wait()
 
 
-def _own_kernel(total, w_in, h_in, t_ref, lse_ref, dwp, x_in, s_in, dwo, dh_ref,
-                w, h, ht, xv, sv, dw, dht, z0, z1, g0, g1, wsem, dsem, osem, lsem):
-    vloc, depth = w_in.shape
-    pieces = _pieces(vloc // SUB, vloc % SUB, UN_L)
+def _own_kernel(total, dwp, w, h, x, s, t_ref, lse_ref, dwo, dh_ref, dw, ht, dht, z0, z1, g0, g1, dsem, osem):
+    vloc = w.shape[0]
     dpieces = _done_pieces(vloc, UN_L)
-    wcopy = [pltpu.make_async_copy(w_in.at[pl.ds(a, n), :], w.at[pl.ds(a, n), :], wsem.at[i]) for i, (a, n) in enumerate(pieces)]
     dcopy = [pltpu.make_async_copy(dwp.at[pl.ds(a, n), :], dw.at[pl.ds(a, n), :], dsem.at[i]) for i, (a, n) in enumerate(dpieces)]
     flush = [pltpu.make_async_copy(dw.at[pl.ds(a, n), :], dwo.at[pl.ds(a, n), :], osem.at[i]) for i, (a, n) in enumerate(dpieces)]
-    own_h = pltpu.make_async_copy(h_in, h, lsem.at[0])
-    recv = [pltpu.make_async_copy(x_in, xv, lsem.at[1]), pltpu.make_async_copy(s_in, sv, lsem.at[2])]
-    own_h.start()
-    wcopy[0].start()
-    for i in range(len(dpieces)):
-        wcopy[i + 1].start()
-        dcopy[i].start()
-    for c in recv:
-        c.start()
-    own_h.wait()
-    ht[...] = h[...].T
-
-    def need(n):
-        wcopy[n].wait()
-        if n > 0:
-            dcopy[n - 1].wait()
 
     def done(n, cond):
         if cond is None:
@@ -358,11 +341,17 @@
         else:
             pl.when(cond)(lambda: flush[n].start())
 
+    for c in dcopy:
+        c.start()
+    ht[...] = h[...].T
+
+    def need(n):
+        if n > 0:
+            dcopy[n - 1].wait()
+
     tgt = t_ref[...] - lax.axis_index("fsdp") * vloc
     _bwd_chunk(w, h, ht, lse_ref, tgt, dw, dht, (z0, z1), (g0, g1), UN_L, need=need, done=done, scale=1.0 / total)
-    for c in recv:
-        c.wait()
-    dh_ref[...] = dht[...].T + (xv[...] + sv[...])
+    dh_ref[...] = dht[...].T + (x[...] + s[...])
     for c in flush:
         c.wait()
 
@@ -381,40 +370,38 @@
         hbm = pl.BlockSpec(memory_space=pl.ANY)
         loc = pl.BlockSpec(memory_space=pltpu.VMEM)
         np_f = len(_pieces(vloc // SUB, vloc % SUB, UN_O))
-        np_b = len(_pieces(vloc // SUB, vloc % SUB, UN_L))
-        nd = len(_done_pieces(vloc, UN_B))
         nl = len(_done_pieces(vloc, UN_L))
         sds = jax.ShapeDtypeStruct
-        dwp, x, s, lse, loss = pl.pallas_call(
+        work = [vm((SUB, tok), f32), vm((SUB, tok), f32), vm((SUB, tok), bf16), vm((SUB, tok), bf16)]
+        nd = len(_done_pieces(vloc, UN_B))
+        dwp, w, h0, x, s, lse, loss = pl.pallas_call(
             lambda *refs: _exchange_kernel(total, *refs),
             in_specs=[hbm, hbm, hbm],
-            out_specs=[hbm, hbm, hbm, loc, loc],
-            out_shape=[sds((vloc, depth), f32), sds((tok, depth), f32), sds((tok, depth), f32), sds((1, tok), f32), sds((1, 128), f32)],
+            out_specs=[hbm] + [loc] * 6,
+            out_shape=[
+                sds((vloc, depth), f32), vm((vloc, depth), bf16), vm((tok, depth), bf16),
+                vm((tok, depth), f32), vm((tok, depth), f32), vm((1, tok), f32), sds((1, 128), f32),
+            ],
             scratch_shapes=[
-                vm((vloc, depth), bf16), vm((groups, tok, depth), bf16), vm((groups, depth, tok), bf16), vm((vloc, depth), f32),
+                vm((vloc, depth), f32), vm((groups - 1, tok, depth), bf16), vm((depth, tok), bf16), vm((groups - 1, depth, tok), bf16),
                 vm((depth, tok), f32), vm((3, tok, depth), f32), vm((2, half, depth), f32),
                 vm((8, 1, half), jnp.int32), vm((32, 1, half), f32), vm((4, 1, 128), f32), vm((4, 1, tok), f32),
-                vm((SUB, tok), f32), vm((SUB, tok), f32), vm((SUB, tok), bf16), vm((SUB, tok), bf16),
-                vm((8, tok), f32), vm((8, tok), f32), vm((8, tok), f32), vm((8, tok), f32), vm((8, tok), f32), vm((8, tok), f32),
+            ] + work + [vm((8, tok), f32)] * 6 + [
                 dma((np_f,)), dma((2,)), dma((5,)), dma((5,)), dma, dma, dma, dma((4,)), dma((5,)), dma((5,)), dma, dma, dma((nd,)),
             ],
-            compiler_params=pltpu.CompilerParams(vmem_limit_bytes=66_500_000, collective_id=0, has_side_effects=True),
+            compiler_params=pltpu.CompilerParams(vmem_limit_bytes=VMEM_X, collective_id=0, has_side_effects=True),
             name="ce_exchange",
         )(hidden, targets.reshape(2, 1, half), weight)
-        dw, dh = pl.pallas_call(
+        keep = lambda a: pltpu.with_memory_space_constraint(a, pltpu.VMEM)
+        grad_w, dh = pl.pallas_call(
             lambda *refs: _own_kernel(total, *refs),
-            in_specs=[hbm, hbm, loc, loc, hbm, hbm, hbm],
+            in_specs=[hbm] + [loc] * 6,
             out_specs=[hbm, loc],
             out_shape=[sds((vloc, depth), f32), sds((tok, depth), f32)],
-            scratch_shapes=[
-                vm((vloc, depth), bf16), vm((tok, depth), bf16), vm((depth, tok), bf16), vm((tok, depth), f32), vm((tok, depth), f32),
-                vm((vloc, depth), f32), vm((depth, tok), f32),
-                vm((SUB, tok), f32), vm((SUB, tok), f32), vm((SUB, tok), bf16), vm((SUB, tok), bf16),
-                dma((np_b,)), dma((nl,)), dma((nl,)), dma((3,)),
-            ],
-            compiler_params=pltpu.CompilerParams(vmem_limit_bytes=66_500_000),
+            scratch_shapes=[vm((vloc, depth), f32), vm((depth, tok), bf16), vm((depth, tok), f32)] + work + [dma((nl,)), dma((nl,))],
+            compiler_params=pltpu.CompilerParams(vmem_limit_bytes=VMEM_L),
             name="ce_own",
-        )(weight, hidden, targets[None, :], lse, dwp, x, s)
-        return loss[0, :1], dh, dw
+        )(dwp, *[keep(a) for a in (w, h0, x, s)], targets[None, :], keep(lse))
+        return loss[0, :1], dh, grad_w
 
     return jax.shard_map(local_head, mesh=mesh, in_specs=(tok_spec, P(("dp", "fsdp")), P("fsdp", None)), out_specs=(P("dp"), tok_spec, tok_spec), check_vma=False)

time: 185 us -> 186 us (level)
    pallas_call x1, Pallas kernels: 145 us -> 151 us  [local_head(): pl.pallas_call(lambda *refs: _exchange_kernel(total, *refs), in_specs=[hb...]
    pallas_call x1, Pallas kernels: 38.6 us -> 33.4 us  [local_head(): pl.pallas_call(lambda *refs: _own_kernel(total, *refs), in_specs=[hbm] +...]
where the time goes in v1:
time: 186 us
  Pallas kernels  184 us (99%)
    pallas_call x1, Pallas kernels, local_head(): pl.pallas_call(lambda *refs: _exchange_kernel(total, *refs), in_specs=[hb...  151 us
    pallas_call x1, Pallas kernels, local_head(): pl.pallas_call(lambda *refs: _own_kernel(total, *refs), in_specs=[hbm] +...  33.4 us

profile of v1, /device:TPU:0, one launch (start us, length us, event | category | flops | bytes accessed | tf_op | source)
XLA Modules:
  0.0 186.2 jit_solution(6745157627978312081)
XLA Ops:
  0.6 0.0 copy-start
  0.6 150.9 %ce_exchange.1 = (f32[8032,512]{1,0:T(8,128)}, bf16[8032,512]{1,0:T(8,128)(2,1)S(1)}, bf16[1024,512]{1,0:T(8,128)(2,1)S(1)}, f32[1024,512]{1,0:T(8,128)S(1)}, f3...) custom-call(bf16[1024,512]{1,0:T(8,128)(2,1)} %refs_0_.1, s32[2,1,512]{2,1,0:T(1,128)} %bitcast.4, ...), custom_call_target="tpu_custom_call" | custom-call | tf_op jit(solution)/shard_map/ce_exchange/pallas_call | solution.py:377
  151.5 0.0 copy-done
  151.5 0.0 copy-start.1
  151.5 33.4 %ce_own.1 = (f32[8032,512]{1,0:T(8,128)}, f32[1024,512]{1,0:T(8,128)}) custom-call(f32[8032,512]{1,0:T(8,128)} %get-tuple-element.13.refs_0_, bf16[8032,512]{1,0:T(8,128)(2,1)S(1)} %get-tuple-element.14.refs_1_, bf16[1024,512]{1,0:T(8,128)(2,1)S(1)} %get-tuple-element.15.refs_2_, f32[1024,512]{1,0:T(8,128)S(1)} %get-tuple-element.16.refs_3_, ...), custom_call_target="tpu_custom_call" | custom-call | tf_op jit(solution)/shard_map/ce_own/pallas_call | solution.py:396
  185.0 0.0 copy-done.1
Async XLA Ops:
  0.6 150.9 %copy-start = (s32[1024]{0:T(1024)S(1)}, s32[1024]{0:T(1024)}, u32[]{:S(2)}) copy-start(s32[1024]{0:T(1024)} %param.4) | copy-start | bytes 12292
  151.5 33.5 %copy-start.1 = (f32[1,128]{1,0:T(1,128)S(1)}, f32[1,128]{1,0:T(1,128)}, u32[]{:S(2)}) copy-start(f32[1,128]{1,0:T(1,128)} %get-tuple-element.12) | copy-start | bytes 1540

commit v2 on v1

--- a/solution.py
+++ b/solution.py
@@ -10,8 +10,8 @@
 UN_F = 14
 UN_B = 14
 UN_L = 4
-VMEM_X = 44_000_000
-VMEM_L = 30_000_000
+VMEM_X = 56_500_000
+VMEM_L = 56_500_000
 f32 = jnp.float32
 bf16 = jnp.bfloat16
 MESH = pl.DeviceIdType.MESH
@@ -93,7 +93,7 @@
     return top + jnp.log(jnp.sum(s8[...] * jnp.exp(m8 - top), axis=0, keepdims=True))
 
 
-def _bwd_chunk(w, h, ht, lse, tgt, dw, dht, zb, gb, un, zt8=None, mid=None, need=None, done=None, scale=1.0):
+def _bwd_chunk(w, h, ht, lse, tgt, dw, dht, zb, gb, un, zt8=None, mid=None, late=None, need=None, done=None, scale=1.0):
     vloc = w.shape[0]
     tok = h.shape[0]
     full, rem = vloc // SUB, vloc % SUB
@@ -139,6 +139,8 @@
                 pl.when(i == n)(lambda n=n: need(1 + n))
         for u in range(un):
             step(1 + i * un + u, (1 + u) % 2)
+        if late is not None:
+            pl.when(i == 0)(late)
         if done is not None:
             for n in range(loops):
                 done(n, i == n)
@@ -289,20 +291,19 @@
         lsec[pl.ds(pos, 1)] = lse[None]
         tpos = jnp.concatenate([tg[pos * 2], tg[pos * 2 + 1]], axis=1) - base
 
-        def combine():
-            for q in range(2):
-                @pl.when(i == q + 1)
-                def _():
-                    swap[q].wait_recv()
-                    for j in range(4):
-                        rows = pl.ds(core * half + j * (half // 4), half // 4)
-                        part[q, rows, :] += ring[q, pl.ds(j * (half // 4), half // 4), :]
-                    cross[q].start()
+        def combine(q):
+            @pl.when(i == q + 1)
+            def _():
+                swap[q].wait_recv()
+                for j in range(4):
+                    rows = pl.ds(core * half + j * (half // 4), half // 4)
+                    part[q, rows, :] += ring[q, pl.ds(j * (half // 4), half // 4), :]
+                cross[q].start()
 
         def done(n, cond):
             pl.when(i == 2 if cond is None else jnp.logical_and(cond, i == 2))(lambda: flush[n].start())
 
-        _bwd_chunk(w, hc.at[pos - 1], ht.at[pos - 1], lse, tpos, dw, dht, zb, gb, UN_B, zt8=zt8, mid=combine, done=done, scale=scale)
+        _bwd_chunk(w, hc.at[pos - 1], ht.at[pos - 1], lse, tpos, dw, dht, zb, gb, UN_B, zt8=zt8, mid=lambda: combine(1), late=lambda: combine(0), done=done, scale=scale)
         part[i] = dht[...].T
         for q in range(2):
             pl.when(i == q)(lambda q=q: swap[q].start())
@@ -329,7 +330,7 @@
         c.wait()
 
 
-def _own_kernel(total, dwp, w, h, x, s, t_ref, lse_ref, dwo, dh_ref, dw, ht, dht, z0, z1, g0, g1, dsem, osem):
+def _own_kernel(total, dwp, w, h, x_in, s_in, t_ref, lse_ref, dwo, dh_ref, dw, x, s, ht, dht, z0, z1, g0, g1, dsem, osem, lsem):
     vloc = w.shape[0]
     dpieces = _done_pieces(vloc, UN_L)
     dcopy = [pltpu.make_async_copy(dwp.at[pl.ds(a, n), :], dw.at[pl.ds(a, n), :], dsem.at[i]) for i, (a, n) in enumerate(dpieces)]
@@ -341,7 +342,8 @@
         else:
             pl.when(cond)(lambda: flush[n].start())
 
-    for c in dcopy:
+    recv = [pltpu.make_async_copy(x_in, x, lsem.at[0]), pltpu.make_async_copy(s_in, s, lsem.at[1])]
+    for c in dcopy + recv:
         c.start()
     ht[...] = h[...].T
 
@@ -351,6 +353,8 @@
 
     tgt = t_ref[...] - lax.axis_index("fsdp") * vloc
     _bwd_chunk(w, h, ht, lse_ref, tgt, dw, dht, (z0, z1), (g0, g1), UN_L, need=need, done=done, scale=1.0 / total)
+    for c in recv:
+        c.wait()
     dh_ref[...] = dht[...].T + (x[...] + s[...])
     for c in flush:
         c.wait()
@@ -377,10 +381,10 @@
         dwp, w, h0, x, s, lse, loss = pl.pallas_call(
             lambda *refs: _exchange_kernel(total, *refs),
             in_specs=[hbm, hbm, hbm],
-            out_specs=[hbm] + [loc] * 6,
+            out_specs=[hbm, loc, loc, hbm, hbm, loc, loc],
             out_shape=[
                 sds((vloc, depth), f32), vm((vloc, depth), bf16), vm((tok, depth), bf16),
-                vm((tok, depth), f32), vm((tok, depth), f32), vm((1, tok), f32), sds((1, 128), f32),
+                sds((tok, depth), f32), sds((tok, depth), f32), vm((1, tok), f32), sds((1, 128), f32),
             ],
             scratch_shapes=[
                 vm((vloc, depth), f32), vm((groups - 1, tok, depth), bf16), vm((depth, tok), bf16), vm((groups - 1, depth, tok), bf16),
@@ -395,13 +399,14 @@
         keep = lambda a: pltpu.with_memory_space_constraint(a, pltpu.VMEM)
         grad_w, dh = pl.pallas_call(
             lambda *refs: _own_kernel(total, *refs),
-            in_specs=[hbm] + [loc] * 6,
+            in_specs=[hbm, loc, loc, hbm, hbm, loc, loc],
             out_specs=[hbm, loc],
             out_shape=[sds((vloc, depth), f32), sds((tok, depth), f32)],
-            scratch_shapes=[vm((vloc, depth), f32), vm((depth, tok), bf16), vm((depth, tok), f32)] + work + [dma((nl,)), dma((nl,))],
+            scratch_shapes=[vm((vloc, depth), f32), vm((tok, depth), f32), vm((tok, depth), f32), vm((depth, tok), bf16), vm((depth, tok), f32)]
+            + work + [dma((nl,)), dma((nl,)), dma((2,))],
             compiler_params=pltpu.CompilerParams(vmem_limit_bytes=VMEM_L),
             name="ce_own",
-        )(dwp, *[keep(a) for a in (w, h0, x, s)], targets[None, :], keep(lse))
+        )(dwp, *[keep(a) for a in (w, h0)], x, s, targets[None, :], keep(lse))
         return loss[0, :1], dh, grad_w
 
     return jax.shard_map(local_head, mesh=mesh, in_specs=(tok_spec, P(("dp", "fsdp")), P("fsdp", None)), out_specs=(P("dp"), tok_spec, tok_spec), check_vma=False)

time: 186 us -> 178 us (0.957)
  Pallas kernels: 184 us -> 176 us
    pallas_call x1, Pallas kernels: 151 us -> 143 us  [local_head(): pl.pallas_call(lambda *refs: _exchange_kernel(total, *refs), in_specs=[hb...]
where the time goes in v2:
time: 178 us; the launch traced here: 177 us
  Pallas kernels  176 us (99%)
  between operations  1.82 us (1%)
    pallas_call x1, Pallas kernels, local_head(): pl.pallas_call(lambda *refs: _exchange_kernel(total, *refs), in_specs=[hb...  143 us
    pallas_call x1, Pallas kernels, local_head(): pl.pallas_call(lambda *refs: _own_kernel(total, *refs), in_specs=[hbm, lo...  32.8 us

profile of v2, /device:TPU:0, one launch (start us, length us, event | category | flops | bytes accessed | tf_op | source)
XLA Modules:
  0.0 177.5 jit_solution(15551806102594694372)
XLA Ops:
  0.6 142.9 %ce_exchange.1 = (f32[8032,512]{1,0:T(8,128)}, bf16[8032,512]{1,0:T(8,128)(2,1)S(1)}, bf16[1024,512]{1,0:T(8,128)(2,1)S(1)}, f32[1024,512]{1,0:T(8,128)}, f32[10...) custom-call(bf16[1024,512]{1,0:T(8,128)(2,1)} %refs_0_.1, s32[2,1,512]{2,1,0:T(1,128)} %bitcast.4, ...), custom_call_target="tpu_custom_call" | custom-call | tf_op jit(solution)/shard_map/ce_exchange/pallas_call | solution.py:381
  143.5 0.0 copy-start
  143.5 32.8 %ce_own.1 = (f32[8032,512]{1,0:T(8,128)}, f32[1024,512]{1,0:T(8,128)}) custom-call(f32[8032,512]{1,0:T(8,128)} %get-tuple-element.13.refs_0_, bf16[8032,512]{1,0:T(8,128)(2,1)S(1)} %get-tuple-element.14.refs_1_, bf16[1024,512]{1,0:T(8,128)(2,1)S(1)} %get-tuple-element.15.refs_2_, f32[1024,512]{1,0:T(8,128)} %get-tuple-element.16.refs_3_, ...), custom_call_target="tpu_custom_call" | custom-call | tf_op jit(solution)/shard_map/ce_own/pallas_call | solution.py:400
  176.3 0.0 copy-done
Async XLA Ops:
  143.5 32.8 %copy-start = (f32[1,128]{1,0:T(1,128)S(1)}, f32[1,128]{1,0:T(1,128)}, u32[]{:S(2)}) copy-start(f32[1,128]{1,0:T(1,128)} %get-tuple-element.12) | copy-start | bytes 1540
